TPU v7x, 8 devices: a whole 2x2x1 slice. The times are simulated.
8 devices in a mesh: tp: 8 (over z, y, x, core).
Axes of the slice: x: 2, y: 2, z: 1, core: 2. Of those that a mesh axis runs over, the one named last changes fastest.
Arguments:
- hidden_in: bfloat16 [12, 768, 4096], P(None, 'tp')
- lengths: int32 [12], replicated
- attn_norm: bfloat16 [2, 4096], replicated
- w_query: bfloat16 [2, 4096, 32, 128], replicated
- w_key: bfloat16 [2, 4096, 8, 128], replicated
- w_value: bfloat16 [2, 4096, 8, 128], replicated
- w_out: bfloat16 [2, 32, 128, 4096], replicated
- mlp_norm: bfloat16 [2, 4096], replicated
- w_gate: bfloat16 [2, 4096, 14336], P(None, None, 'tp')
- w_up: bfloat16 [2, 4096, 14336], P(None, None, 'tp')
- w_down: bfloat16 [2, 14336, 4096], P(None, 'tp')
- final_norm: bfloat16 [4096], replicated
Outputs:
- output: bfloat16 [12, 768, 4096], P(None, 'tp')
All inputs are finite; a program needn't handle non-finite values.
Results may differ from a plain program's by a relative error of at most 0.02.
Values are sent between devices in bfloat16 or wider.
A program may use at most 1.25 GiB of HBM per device.

v0:
```python
import jax
import jax.numpy as jnp
from jax import lax
from jax.sharding import PartitionSpec as P

NORM_EPS = 1e-5
ROPE_BASE = 500000.0


def rms_norm(hidden, gain):
    h_wide = hidden.astype(jnp.float32)
    inv_rms = lax.rsqrt(jnp.mean(h_wide * h_wide, axis=-1, keepdims=True) + NORM_EPS)
    return (h_wide * inv_rms * gain.astype(jnp.float32)).astype(jnp.bfloat16)


def rope_tables(positions, head_dim):
    half_dim = head_dim // 2
    inv_freq = ROPE_BASE ** (-2.0 * jnp.arange(half_dim).astype(jnp.float32) / head_dim)
    angles = positions.astype(jnp.float32)[:, None, None] * inv_freq[None, None, :]
    return jnp.cos(angles), jnp.sin(angles)


def rotate(proj, cos_tab, sin_tab):
    half_dim = proj.shape[-1] // 2
    first = proj[..., :half_dim]
    second = proj[..., half_dim:]
    return jnp.concatenate([first * cos_tab - second * sin_tab, second * cos_tab + first * sin_tab], axis=-1)


def attend(q_rot, k_all, v_all, q_pos, lengths):
    head_dim = q_rot.shape[-1]
    key_pos = jnp.arange(k_all.shape[1])
    allowed = (key_pos[None, None, :] <= q_pos[None, :, None]) & (key_pos[None, None, :] < lengths[:, None, None])
    scores = jnp.einsum('bqkgd,bskd->bkgqs', q_rot, k_all, preferred_element_type=jnp.float32) * (head_dim ** -0.5)
    scores = jnp.where(allowed[:, None, None, :, :], scores, -1e30)
    prob_mat = jax.nn.softmax(scores, axis=-1).astype(jnp.bfloat16)
    context = jnp.einsum('bkgqs,bskd->bqkgd', prob_mat, v_all, preferred_element_type=jnp.float32)
    return context.astype(jnp.bfloat16)


def solution(mesh):
    tp_size = mesh.shape['tp']

    def device_fn(hidden_in, lengths, attn_norm, w_query, w_key, w_value, w_out, mlp_norm, w_gate, w_up, w_down, final_norm):
        batch, seq_dev, d_model = hidden_in.shape
        heads = w_query.shape[2]
        head_dim = w_query.shape[3]
        kv_heads = w_key.shape[2]
        groups = heads // kv_heads
        q_pos = lax.axis_index('tp') * seq_dev + jnp.arange(seq_dev)
        cos_tab, sin_tab = rope_tables(q_pos, head_dim)
        hidden = hidden_in
        for layer in range(w_query.shape[0]):
            normed = rms_norm(hidden, attn_norm[layer])
            q_proj = jnp.einsum('bsd,dhe->bshe', normed, w_query[layer], preferred_element_type=jnp.float32)
            k_proj = jnp.einsum('bsd,dhe->bshe', normed, w_key[layer], preferred_element_type=jnp.float32)
            v_proj = jnp.einsum('bsd,dhe->bshe', normed, w_value[layer], preferred_element_type=jnp.float32).astype(jnp.bfloat16)
            q_rot = rotate(q_proj, cos_tab, sin_tab).astype(jnp.bfloat16).reshape(batch, seq_dev, kv_heads, groups, head_dim)
            k_rot = rotate(k_proj, cos_tab, sin_tab).astype(jnp.bfloat16)
            k_all = lax.all_gather(k_rot, 'tp', axis=1, tiled=True)
            v_all = lax.all_gather(v_proj, 'tp', axis=1, tiled=True)
            context = attend(q_rot, k_all, v_all, q_pos, lengths).reshape(batch, seq_dev, heads, head_dim)
            attn_out = jnp.einsum('bshe,hed->bsd', context, w_out[layer], preferred_element_type=jnp.float32)
            hidden = (hidden.astype(jnp.float32) + attn_out).astype(jnp.bfloat16)
            normed = rms_norm(hidden, mlp_norm[layer])
            full_normed = lax.all_gather(normed, 'tp', axis=1, tiled=True)
            gate_proj = jnp.einsum('bsd,df->bsf', full_normed, w_gate[layer], preferred_element_type=jnp.float32)
            up_proj = jnp.einsum('bsd,df->bsf', full_normed, w_up[layer], preferred_element_type=jnp.float32)
            gated_act = (jax.nn.silu(gate_proj) * up_proj).astype(jnp.bfloat16)
            part_out = jnp.einsum('bsf,fd->bsd', gated_act, w_down[layer], preferred_element_type=jnp.float32).astype(jnp.bfloat16)
            part_out = part_out.reshape(batch, tp_size, seq_dev, d_model)
            received = lax.all_to_all(part_out, 'tp', 1, 1, tiled=True)
            mlp_out = jnp.sum(received, axis=1, dtype=jnp.float32)
            hidden = (hidden.astype(jnp.float32) + mlp_out).astype(jnp.bfloat16)
        return rms_norm(hidden, final_norm)

    seq_part = P(None, 'tp', None)
    in_specs = (seq_part, P(), P(), P(), P(), P(), P(), P(), P(None, None, 'tp'), P(None, None, 'tp'), P(None, 'tp', None), P())
    return jax.shard_map(device_fn, mesh=mesh, in_specs=in_specs, out_specs=seq_part, check_vma=False)
```

profile of v0, /device:TPU:0, one launch (start us, length us, event | category | flops | bytes accessed | tf_op | source)
XLA Modules:
  0.0 4262.0 jit_solution(13721496107210862021)
XLA Ops:
  25.3 15.0 fusion.72
  54.2 13.6 fusion.83
  70.1 43.7 %fusion.103 = (bf16[1,4096,32,128]{3,2,1,0:T(8,128)(2,1)}, bf16[1,4096,32,128]{3,2,1,0:T(8,128)(2,1)}) fusion(bf16[2,4096,32,128]{3,2,1,0:T(8,128)(2,1)} %param.15), kind=kLoop, calls=%fused_computation.142 | loop fusion | bytes 134217728 | tf_op jit(solution)/shard_map/slice | solution.py:55
  113.8 48.4 %fusion.13 = f32[12,96,32,128]{3,1,2,0:T(8,128)} fusion(bf16[1,4096,32,128]{3,2,1,0:T(8,128)(2,1)} %get-tuple-element.8, bf16[12,96,4096]{2,1,0:T(8,128)(2,1)} %param.12, f32[4096]{0:T(1024)S(1)} %bitcast.192, f32[12,96]{1,0:T(8,128)S(1)} %add_rsqrt_fusion.4), kind=kOutput, calls=%fused_computation.27 | convolution fusion | flops 38673580032 | bytes 61886976 | tf_op jit(solution)/shard_map/bsd,dhe->bshe/dot_general | solution.py:55
  162.3 20.2 subtract_convert_fusion.1
  182.5 51.1 %fusion.42 = f32[12,8,768,96,4]{2,3,4,1,0:T(8,128)} fusion(bf16[12,768,8,128]{3,1,2,0:T(8,128)(2,1)} %all-gather.9.cloned.1.call-done, bf16[12,96,8,4,64]{4,1,3,2,0:T(8,128)(2,1)} %bitcast.184, bf16[12,96,8,4,64]{4,1,3,2,0:T(8,128)(2,1)} %bitcast.183), kind=kOutput, calls=%fused_computation.70 | convolution fusion | flops 7266631680 | bytes 141557760 | tf_op jit(solution)/shard_map/bqkgd,bskd->bkgqs/dot_general | solution.py:34
  233.6 112.8 %fusion.105 = (f32[12,8,4,96]{3,2,1,0:T(4,128)S(1)}, f32[12,8,4,96,768]{4,3,2,1,0:T(8,128)}) fusion(f32[12,8,768,96,4]{2,3,4,1,0:T(8,128)} %fusion.42, pred[12,96,768]{2,1,0:T(8,128)(4,1)S(1)} %copy-done.7), kind=kOutput, calls=%fused_computation.144 | output fusion | flops 169870080 | bytes 227524608 | tf_op jit(solution)/shard_map/sub | solution.py:36
  346.4 44.9 %fusion.80 = bf16[12,8,128,4,96]{2,4,3,1,0:T(8,128)(2,1)} fusion(f32[12,8,4,96,768]{4,3,2,1,0:T(8,128)} %get-tuple-element.28, f32[12,8,4,96]{3,2,1,0:T(4,128)S(1)} %get-tuple-element.27, bf16[12,768,8,128]{3,1,2,0:T(8,128)(2,1)} %all-gather.7.cloned.1.call-done), kind=kOutput, calls=%fused_computation.110 | convolution fusion | flops 7309099008 | bytes 141705216 | tf_op jit(solution)/shard_map/bkgqs,bskd->bqkgd/dot_general | solution.py:37
  391.3 48.5 %fusion.27 = (f32[12,96]{1,0:T(8,128)S(1)}, bf16[12,96,4096]{2,1,0:T(8,128)(2,1)}) fusion(bf16[12,96,32,128]{3,1,2,0:T(8,128)(2,1)} %bitcast.194, bf16[2,32,128,4096]{3,2,1,0:T(8,128)(2,1)} %param.18, bf16[12,96,4096]{2,1,0:T(8,128)(2,1)} %param.12), kind=kOutput, calls=%fused_computation.55 | convolution fusion | flops 38683017216 | bytes 61870592 | tf_op jit(solution)/shard_map/bshe,hed->bsd/dot_general | solution.py:63
  439.8 11.4 fusion.29
  451.3 336.3 %all-gather.11.cloned.1.call-done = bf16[12,768,4096]{2,1,0:T(8,128)(2,1)} async-done(((bf16[12,96,4096]{2,1,0:T(8,128)(2,1)}), bf16[12,768,4096]{2,1,0:T(8,128)(2,1)}) %all-gather.11.cloned.1.call-update) | async-done | bytes 75497488 | tf_op jit(solution)/shard_map/all_gather | solution.py:66
  787.6 148.3 %fusion.50 = f32[12,768,1792]{2,1,0:T(8,128)} fusion(bf16[12,768,4096]{2,1,0:T(8,128)(2,1)} %all-gather.11.cloned.1.call-done, bf16[2,4096,1792]{2,1,0:T(8,128)(2,1)} %param.21), kind=kOutput, calls=%fused_computation.82 | convolution fusion | flops 135291469824 | bytes 156237824 | tf_op jit(solution)/shard_map/bsd,df->bsf/dot_general | solution.py:68
  935.9 154.6 %multiply_convert_fusion.1 = bf16[12,768,1792]{2,1,0:T(8,128)(2,1)} fusion(f32[12,768,1792]{2,1,0:T(8,128)} %fusion.50, bf16[12,768,4096]{2,1,0:T(8,128)(2,1)} %all-gather.11.cloned.1.call-done, bf16[2,4096,1792]{2,1,0:T(8,128)(2,1)} %param.20), kind=kOutput, calls=%fused_computation.13 | convolution fusion | flops 135390560256 | bytes 189267968 | tf_op jit(solution)/shard_map/bsd,df->bsf/dot_general | solution.py:67
  1090.6 147.1 %convolution_convert_fusion.1 = bf16[12,768,4096]{2,1,0:T(8,128)(2,1)} fusion(bf16[12,768,1792]{2,1,0:T(8,128)(2,1)} %multiply_convert_fusion.1, bf16[2,1792,4096]{2,1,0:T(8,128)(2,1)} %param.22), kind=kOutput, calls=%fused_computation.23 | convolution fusion | flops 135329218560 | bytes 123207680 | tf_op jit(solution)/shard_map/bsf,fd->bsd/dot_general | solution.py:70
  1237.7 49.1 %copy.19 = bf16[12,8,96,4096]{3,2,0,1:T(8,128)(2,1)} copy(bf16[12,8,96,4096]{3,2,1,0:T(8,128)(2,1)} %bitcast.30) | data formatting | bytes 150994944 | tf_op jit(solution)/shard_map/reshape | solution.py:71
  1286.8 831.8 %all_to_all.10 = bf16[12,8,96,4096]{3,2,0,1:T(8,128)(2,1)} all-to-all(bf16[12,8,96,4096]{3,2,0,1:T(8,128)(2,1)} %copy.19), channel_id=1, replica_groups=mesh['tp'=8] {'tp'}, dimensions={1} | all-to-all | bytes 150994944 | tf_op jit(solution)/shard_map/all_to_all | solution.py:72
  2118.6 38.8 convert_reduce_fusion.1
  2167.2 12.6 fusion.71
  2184.5 16.0 fusion.86
  2200.6 48.8 %fusion.12 = f32[12,96,32,128]{3,1,2,0:T(8,128)} fusion(bf16[1,4096,32,128]{3,2,1,0:T(8,128)(2,1)} %get-tuple-element.7, bf16[12,96,4096]{2,1,0:T(8,128)(2,1)} %get-tuple-element.6, f32[4096]{0:T(1024)S(1)} %bitcast.189, f32[12,96]{1,0:T(8,128)S(1)} %copy-done.15), kind=kOutput, calls=%fused_computation.25 | convolution fusion | flops 38673580032 | bytes 61886976 | tf_op jit(solution)/shard_map/bsd,dhe->bshe/dot_general | solution.py:55
  2249.5 20.3 subtract_convert_fusion
  2276.6 50.9 %fusion.39 = f32[12,8,768,96,4]{2,3,4,1,0:T(8,128)} fusion(bf16[12,768,8,128]{3,1,2,0:T(8,128)(2,1)} %all-gather.15.cloned.1.call-done, bf16[12,96,8,4,64]{4,1,3,2,0:T(8,128)(2,1)} %bitcast.182, bf16[12,96,8,4,64]{4,1,3,2,0:T(8,128)(2,1)} %bitcast.181), kind=kOutput, calls=%fused_computation.67 | convolution fusion | flops 7266631680 | bytes 141557760 | tf_op jit(solution)/shard_map/bqkgd,bskd->bkgqs/dot_general | solution.py:34
  2327.6 112.9 %fusion.106 = (f32[12,8,4,96]{3,2,1,0:T(4,128)S(1)}, f32[12,8,4,96,768]{4,3,2,1,0:T(8,128)}) fusion(f32[12,8,768,96,4]{2,3,4,1,0:T(8,128)} %fusion.39, pred[12,96,768]{2,1,0:T(8,128)(4,1)S(1)} %copy-done.8), kind=kOutput, calls=%fused_computation.145 | output fusion | flops 169870080 | bytes 227524608 | tf_op jit(solution)/shard_map/sub | solution.py:36
  2440.5 45.0 %fusion.77 = bf16[12,8,128,4,96]{2,4,3,1,0:T(8,128)(2,1)} fusion(f32[12,8,4,96,768]{4,3,2,1,0:T(8,128)} %get-tuple-element.32, f32[12,8,4,96]{3,2,1,0:T(4,128)S(1)} %get-tuple-element.31, bf16[12,768,8,128]{3,1,2,0:T(8,128)(2,1)} %all-gather.13.cloned.1.call-done), kind=kOutput, calls=%fused_computation.109 | convolution fusion | flops 7309099008 | bytes 141705216 | tf_op jit(solution)/shard_map/bkgqs,bskd->bqkgd/dot_general | solution.py:37
  2485.5 47.9 %fusion.35 = (f32[12,96]{1,0:T(8,128)S(1)}, bf16[12,96,4096]{2,1,0:T(8,128)(2,1)}) fusion(bf16[12,96,32,128]{3,1,2,0:T(8,128)(2,1)} %bitcast.193, bf16[2,32,128,4096]{3,2,1,0:T(8,128)(2,1)} %param.18, bf16[12,96,4096]{2,1,0:T(8,128)(2,1)} %get-tuple-element.6), kind=kOutput, calls=%fused_computation.63 | convolution fusion | flops 38683017216 | bytes 61870592 | tf_op jit(solution)/shard_map/bshe,hed->bsd/dot_general | solution.py:63
  2544.8 333.4 %all-gather.17.cloned.1.call-done = bf16[12,768,4096]{2,1,0:T(8,128)(2,1)} async-done(((bf16[12,96,4096]{2,1,0:T(8,128)(2,1)}), bf16[12,768,4096]{2,1,0:T(8,128)(2,1)}) %all-gather.17.cloned.1.call-update) | async-done | bytes 75497488 | tf_op jit(solution)/shard_map/all_gather | solution.py:66
  2878.3 148.6 %fusion.46 = f32[12,768,1792]{2,1,0:T(8,128)} fusion(bf16[12,768,4096]{2,1,0:T(8,128)(2,1)} %all-gather.17.cloned.1.call-done, bf16[2,4096,1792]{2,1,0:T(8,128)(2,1)} %param.21), kind=kOutput, calls=%fused_computation.78 | convolution fusion | flops 135291469824 | bytes 156237824 | tf_op jit(solution)/shard_map/bsd,df->bsf/dot_general | solution.py:68
  3026.9 154.4 %multiply_convert_fusion = bf16[12,768,1792]{2,1,0:T(8,128)(2,1)} fusion(f32[12,768,1792]{2,1,0:T(8,128)} %fusion.46, bf16[12,768,4096]{2,1,0:T(8,128)(2,1)} %all-gather.17.cloned.1.call-done, bf16[2,4096,1792]{2,1,0:T(8,128)(2,1)} %param.20), kind=kOutput, calls=%fused_computation.12 | convolution fusion | flops 135390560256 | bytes 189267968 | tf_op jit(solution)/shard_map/bsd,df->bsf/dot_general | solution.py:67
  3181.3 147.1 %convolution_convert_fusion = bf16[12,768,4096]{2,1,0:T(8,128)(2,1)} fusion(bf16[12,768,1792]{2,1,0:T(8,128)(2,1)} %multiply_convert_fusion, bf16[2,1792,4096]{2,1,0:T(8,128)(2,1)} %param.22), kind=kOutput, calls=%fused_computation.22 | convolution fusion | flops 135329218560 | bytes 123207680 | tf_op jit(solution)/shard_map/bsf,fd->bsd/dot_general | solution.py:70
  3328.4 49.1 %copy.22 = bf16[12,8,96,4096]{3,2,0,1:T(8,128)(2,1)} copy(bf16[12,8,96,4096]{3,2,1,0:T(8,128)(2,1)} %bitcast.61) | data formatting | bytes 150994944 | tf_op jit(solution)/shard_map/reshape | solution.py:71
  3387.2 813.7 %all-to-all-done.1 = bf16[12,8,96,4096]{3,2,0,1:T(8,128)(2,1)} async-done(((bf16[12,8,96,4096]{3,2,0,1:T(8,128)(2,1)}), bf16[12,8,96,4096]{3,2,0,1:T(8,128)(2,1)}, u32[]{:S(2)}, u32[]{:S(2)}) %all-to-all-start.1) | async-done | bytes 75497504 | tf_op jit(solution)/shard_map/all_to_all | solution.py:72
  4201.0 38.8 convert_reduce_fusion
  (76 shorter events, 92.5 us)
Async XLA Ops:
  6.5 175.9 %all-gather.9.cloned.1.call-start = ((), (), s32[]{:S(2)}) async-start(), calls=%async_computation.3 | async-start | bytes 21233664 | tf_op jit(solution)/shard_map/all_gather | solution.py:60
  25.3 15.1 copy-start.1
  25.3 15.1 copy-start.4
  44.9 301.4 %all-gather.7.cloned.1.call-start = ((), (), s32[]{:S(2)}) async-start(), calls=%async_computation.2 | async-start | bytes 21233664 | tf_op jit(solution)/shard_map/all_gather | solution.py:61
  54.2 13.8 copy-start.16
  54.2 13.9 copy-start.11
  67.9 719.7 %all-gather.11.cloned.1.call-start = ((), (), s32[]{:S(2)}) async-start(), calls=%async_computation.4 | async-start | bytes 84934656 | tf_op jit(solution)/shard_map/all_gather | solution.py:66
  113.8 48.4 %copy-start.2 = (f32[96,64]{1,0:T(8,128)S(1)}, f32[96,64]{1,0:T(8,128)}, u32[]{:S(2)}) copy-start(f32[96,64]{1,0:T(8,128)} %copy-done.1) | copy-start | bytes 73732
  113.8 48.4 %copy-start.5 = (f32[96,64]{1,0:T(8,128)S(1)}, f32[96,64]{1,0:T(8,128)}, u32[]{:S(2)}) copy-start(f32[96,64]{1,0:T(8,128)} %copy-done.4) | copy-start | bytes 73732
  182.5 51.1 %copy-start.7 = (pred[12,96,768]{2,1,0:T(8,128)(4,1)S(1)}, pred[12,96,768]{2,1,0:T(8,128)(4,1)}, u32[]{:S(2)}) copy-start(pred[12,96,768]{2,1,0:T(8,128)(4,1)} %broadcast_and_fusion) | copy-start | bytes 2654212
  391.3 48.5 %copy-start.10 = (f32[1,4096]{1,0:T(1,128)S(1)}, f32[1,4096]{1,0:T(1,128)}, u32[]{:S(2)}) copy-start(f32[1,4096]{1,0:T(1,128)} %get-tuple-element.22) | copy-start | bytes 49156
  451.3 1825.4 %all-gather.15.cloned.1.call-start = ((), (), s32[]{:S(2)}) async-start(), calls=%async_computation.6 | async-start | bytes 21233664 | tf_op jit(solution)/shard_map/all_gather | solution.py:60
  2157.4 9.8 copy-start
  2167.2 12.6 copy-start.14
  2167.2 12.6 copy-start.3
  2167.2 12.6 copy-start.6
  2179.8 4.6 copy-start.12
  2184.4 256.1 %all-gather.13.cloned.1.call-start = ((), (), s32[]{:S(2)}) async-start(), calls=%async_computation.5 | async-start | bytes 21233664 | tf_op jit(solution)/shard_map/all_gather | solution.py:61
  2184.5 16.1 copy-start.15
  2200.6 677.7 %all-gather.17.cloned.1.call-start = ((), (), s32[]{:S(2)}) async-start(), calls=%async_computation.7 | async-start | bytes 84934656 | tf_op jit(solution)/shard_map/all_gather | solution.py:66
  2276.6 50.9 %copy-start.8 = (pred[12,96,768]{2,1,0:T(8,128)(4,1)S(1)}, pred[12,96,768]{2,1,0:T(8,128)(4,1)}, u32[]{:S(2)}) copy-start(pred[12,96,768]{2,1,0:T(8,128)(4,1)} %broadcast_and_fusion) | copy-start | bytes 2654212
  2485.5 47.9 %copy-start.9 = (f32[1,4096]{1,0:T(1,128)S(1)}, f32[1,4096]{1,0:T(1,128)}, u32[]{:S(2)}) copy-start(f32[1,4096]{1,0:T(1,128)} %get-tuple-element.21) | copy-start | bytes 49156
  3377.5 9.7 copy-start.13
  3377.5 823.5 %all-to-all-start.1 = ((bf16[12,8,96,4096]{3,2,0,1:T(8,128)(2,1)}), bf16[12,8,96,4096]{3,2,0,1:T(8,128)(2,1)}, u32[]{:S(2)}, u32[]{:S(2)}) async-start(bf16[12,8,96,4096]{3,2,0,1:T(8,128)(2,1)} %copy.22), calls=%async_computation.1 | async-start | bytes 150994944 | tf_op jit(solution)/shard_map/all_to_all | solution.py:72
Sparse Core Ops, SparseCore 0:
  45.0 95.8 all-gather.8
  142.7 92.9 all-gather.6
  451.4 336.1 all-gather.10
  2184.5 92.0 all-gather.14
  2278.3 92.9 all-gather.12
  2544.9 333.2 all-gather.16
where the time goes:
time: 4270 us; the launch traced here: 4260 us
  waiting for transfers between devices  1490 us (35%)
  matrix products  1340 us (31%)
  blocking collectives  832 us (19%)
  other arithmetic  410 us (10%)
  local copies, waits for them, and re-layouts  162 us (4%)
    all_to_all x1, blocking collectives, device_fn(): received = lax.all_to_all(part_out, 'tp', 1, 1, tiled=True)  832 us
    all_to_all x1, waiting for transfers between devices, device_fn(): received = lax.all_to_all(part_out, 'tp', 1, 1, tiled=True)  814 us
    all_gather x2, waiting for transfers between devices, device_fn(): full_normed = lax.all_gather(normed, 'tp', axis=1, tiled=True)  670 us
    dot_general x2, matrix products, device_fn(): jnp.einsum('bsd,df->bsf', full_normed, w_gate[layer], preferred_element_t...  309 us
    dot_general x2, matrix products, device_fn(): jnp.einsum('bsd,df->bsf', full_normed, w_up[layer], preferred_element_typ...  297 us
    dot_general x2, matrix products, device_fn(): jnp.einsum('bsf,fd->bsd', gated_act, w_down[layer], preferred_element_typ...  294 us
    sub x2, other arithmetic, attend(): prob_mat = jax.nn.softmax(scores, axis=-1).astype(jnp.bfloat16)  226 us
    dot_general x2, matrix products, attend(): jnp.einsum('bqkgd,bskd->bkgqs', q_rot, k_all, preferred_element_type=jnp....  102 us
  transfers between devices with their start and end apart: 7, of which 4 were waited for; matrix products, arithmetic and copies ran while one was open for 13% of the time, Pallas kernels for 0%

commit v1 on v0

v1 whole, which is shorter than its diff:
```python
import functools

import jax
import jax.numpy as jnp
from jax import lax
from jax.experimental import pallas as pl
from jax.experimental.pallas import tpu as pltpu
from jax.sharding import PartitionSpec as P

NORM_EPS = 1e-5
ROPE_BASE = 500000.0


def rms_norm(hidden, gain):
    h_wide = hidden.astype(jnp.float32)
    inv_rms = lax.rsqrt(jnp.mean(h_wide * h_wide, axis=-1, keepdims=True) + NORM_EPS)
    return (h_wide * inv_rms * gain.astype(jnp.float32)).astype(jnp.bfloat16)


def rope_tables(positions, head_dim):
    half_dim = head_dim // 2
    inv_freq = ROPE_BASE ** (-2.0 * jnp.arange(half_dim).astype(jnp.float32) / head_dim)
    angles = positions.astype(jnp.float32)[:, None, None] * inv_freq[None, None, :]
    return jnp.cos(angles), jnp.sin(angles)


def rotate(proj, cos_tab, sin_tab):
    half_dim = proj.shape[-1] // 2
    first = proj[..., :half_dim]
    second = proj[..., half_dim:]
    return jnp.concatenate([first * cos_tab - second * sin_tab, second * cos_tab + first * sin_tab], axis=-1)


def norm_kernel(h_ref, gain_ref, z_ref):
    z_ref[0] = rms_norm(h_ref[0], gain_ref[...])


def norm_rows(blocks, gain, major):
    n, rows, width = blocks.shape
    minor = n // major
    return pl.pallas_call(
        norm_kernel,
        grid=(n,),
        in_specs=[
            pl.BlockSpec((1, rows, width), lambda i: ((i % minor) * major + i // minor, 0, 0)),
            pl.BlockSpec((1, width), lambda i: (0, 0)),
        ],
        out_specs=pl.BlockSpec((1, rows, width), lambda i: (i, 0, 0)),
        out_shape=jax.ShapeDtypeStruct(blocks.shape, jnp.bfloat16),
        cost_estimate=pl.CostEstimate(flops=40 * n * rows * width, bytes_accessed=4 * n * rows * width, transcendentals=0),
        name="norm_rows",
    )(blocks, gain.reshape(1, width))


def attend_kernel(groups, head_dim, q_start, k_start, lens, q_ref, ka_ref, kb_ref, va_ref, vb_ref, c_ref):
    blk = pl.program_id(1)
    rows = q_ref.shape[0]
    keys = ka_ref.shape[1]
    q_all = jnp.concatenate([q_ref[:, g * head_dim:(g + 1) * head_dim] for g in range(groups)], axis=0)
    shape = (groups, rows, keys)
    q_pos = q_start[blk] + lax.broadcasted_iota(jnp.int32, shape, 1).reshape(groups * rows, keys)
    k_off = lax.broadcasted_iota(jnp.int32, (groups * rows, keys), 1)
    last = jnp.minimum(q_pos, lens[blk] - 1)

    def score(k_ref, start):
        s = lax.dot_general(q_all, k_ref[0], (((1,), (1,)), ((), ())), preferred_element_type=jnp.float32)
        return jnp.where(k_off + start <= last, s * (head_dim ** -0.5), -1e30)

    s_a = score(ka_ref, k_start[0])
    s_b = score(kb_ref, k_start[1])
    top = jnp.maximum(jnp.max(s_a, axis=-1, keepdims=True), jnp.max(s_b, axis=-1, keepdims=True))
    e_a = jnp.exp(s_a - top)
    e_b = jnp.exp(s_b - top)
    inv = 1.0 / (jnp.sum(e_a, axis=-1, keepdims=True) + jnp.sum(e_b, axis=-1, keepdims=True))
    ctx = jnp.dot((e_a * inv).astype(jnp.bfloat16), va_ref[0], preferred_element_type=jnp.float32)
    ctx += jnp.dot((e_b * inv).astype(jnp.bfloat16), vb_ref[0], preferred_element_type=jnp.float32)
    ctx = ctx.astype(jnp.bfloat16)
    for g in range(groups):
        c_ref[:, g * head_dim:(g + 1) * head_dim] = ctx[g * rows:(g + 1) * rows]


def attend(q_rot, kv_pair, parts, rows, q_start, k_start, lens, groups, head_dim):
    tokens, width = q_rot.shape
    n_blk = tokens // rows
    kv_heads = width // (groups * head_dim)
    keys = kv_pair[0].shape[1] // parts

    def kv_spec(half, first):
        def index(j, i, *_):
            return (i if parts == 2 else 0, half if parts == 2 else 0, first + j)
        return pl.BlockSpec((1, keys, head_dim), index)

    return pl.pallas_call(
        functools.partial(attend_kernel, groups, head_dim),
        grid_spec=pltpu.PrefetchScalarGridSpec(
            num_scalar_prefetch=3,
            grid=(kv_heads, n_blk),
            in_specs=[pl.BlockSpec((rows, groups * head_dim), lambda j, i, *_: (i, j)), kv_spec(0, 0), kv_spec(1, 0), kv_spec(0, kv_heads), kv_spec(1, kv_heads)],
            out_specs=pl.BlockSpec((rows, groups * head_dim), lambda j, i, *_: (i, j)),
        ),
        out_shape=jax.ShapeDtypeStruct(q_rot.shape, jnp.bfloat16),
        cost_estimate=pl.CostEstimate(flops=32 * tokens * width * keys, bytes_accessed=8 * tokens * width, transcendentals=0),
        name="attend",
    )(q_start, k_start, lens, q_rot, kv_pair[0], kv_pair[1], kv_pair[0], kv_pair[1])


def solution(mesh):
    n_dev = mesh.shape['tp']
    n_chip = n_dev // 2
    swap = [(d, d ^ 1) for d in range(n_dev)]

    def device_fn(hidden_in, lengths, attn_norm, w_query, w_key, w_value, w_out, mlp_norm, w_gate, w_up, w_down, final_norm):
        batch, seq_dev, d_model = hidden_in.shape
        heads, head_dim = w_query.shape[2], w_query.shape[3]
        kv_heads = w_key.shape[2]
        groups = heads // kv_heads
        n_stream = batch // n_chip
        quarter = n_dev // 2
        half_len = quarter * seq_dev
        me = lax.axis_index('tp')
        chip, side = me // 2, me % 2

        def project(hidden, weights, gain, q_pos):
            w_q, w_k, w_v = weights
            tokens = hidden.shape[0]
            cos_tab, sin_tab = rope_tables(q_pos, head_dim)
            normed = rms_norm(hidden, gain)
            k_proj = jnp.einsum('td,dhe->the', normed, w_k, preferred_element_type=jnp.float32)
            k_rot = rotate(k_proj, cos_tab, sin_tab).astype(jnp.bfloat16).reshape(tokens, -1)
            v_proj = jnp.einsum('td,dhe->the', normed, w_v, preferred_element_type=jnp.float32)
            v_proj = v_proj.astype(jnp.bfloat16).reshape(tokens, -1)
            q_proj = jnp.einsum('td,dhe->the', normed, w_q, preferred_element_type=jnp.float32)
            q_rot = rotate(q_proj, cos_tab, sin_tab).astype(jnp.bfloat16).reshape(tokens, -1)
            return q_rot, jnp.concatenate([k_rot, v_proj], axis=-1)

        def add_out(hidden, context, w_mat):
            w_mat = w_mat.reshape(heads * head_dim, d_model)
            attn_out = jnp.dot(context, w_mat, preferred_element_type=jnp.float32)
            return (hidden.astype(jnp.float32) + attn_out).astype(jnp.bfloat16)

        def mlp(gathered, layer, major):
            normed = norm_rows(gathered, mlp_norm[layer], major).reshape(-1, d_model)
            gate_proj = jnp.dot(normed, w_gate[layer], preferred_element_type=jnp.float32)
            up_proj = jnp.dot(normed, w_up[layer], preferred_element_type=jnp.float32)
            gated_act = (jax.nn.silu(gate_proj) * up_proj).astype(jnp.bfloat16)
            part_out = jnp.dot(gated_act, w_down[layer], preferred_element_type=jnp.float32)
            part_out = lax.reduce_precision(part_out, 8, 7)
            return lax.psum_scatter(part_out.reshape(n_dev, -1, d_model), 'tp', scatter_dimension=0, tiled=False)

        pos0 = jnp.tile(me * seq_dev + jnp.arange(seq_dev), n_chip)
        start0 = jnp.broadcast_to(me * seq_dev, (n_chip,)).astype(jnp.int32)
        pos1 = side * half_len + jnp.arange(half_len)
        start1 = (side * half_len + seq_dev * jnp.arange(quarter)).astype(jnp.int32)
        keys0 = (half_len * jnp.arange(2)).astype(jnp.int32)
        keys1 = jnp.stack([side * half_len, (1 - side) * half_len]).astype(jnp.int32)
        hid = hidden_in.reshape(n_chip, n_stream, seq_dev, d_model)
        lens = lengths.reshape(n_chip, n_stream)
        streams = range(n_stream)

        hidden = [hid[:, g].reshape(n_chip * seq_dev, d_model) for g in streams]
        weights = (w_query[0], w_key[0], w_value[0])
        qkv = [project(hidden[g], weights, attn_norm[0], pos0) for g in streams]
        wide = []
        for g in streams:
            q_rot, kv_own = qkv[g]
            kv_all = lax.all_gather(kv_own.reshape(n_chip, seq_dev, -1), 'tp', axis=1, tiled=True)
            context = attend(q_rot, (kv_all, kv_all), 2, seq_dev, start0, keys0, lens[:, g], groups, head_dim)
            hidden[g] = add_out(hidden[g], context, w_out[0])
            wide.append(lax.all_gather(hidden[g], 'tp', axis=0, tiled=True).reshape(n_dev * n_chip, seq_dev, d_model))

        total = [mlp(wide[g], 0, n_chip) for g in streams]
        before = None
        later = lax.optimization_barrier((w_query, w_key, w_value, w_out, wide[-1]))
        weights = tuple(w[1] for w in later[:4])
        for g in streams:
            if before is not None:
                total[g] = lax.optimization_barrier((total[g], before))[0]
            mine = lax.dynamic_slice(wide[g].reshape(2, quarter, n_chip, seq_dev, d_model), (side, 0, chip, 0, 0), (1, quarter, 1, seq_dev, d_model))
            hidden[g] = (mine.reshape(half_len, d_model).astype(jnp.float32) + total[g]).astype(jnp.bfloat16)
            q_rot, kv_own = project(hidden[g], weights[:3], attn_norm[1], pos1)
            kv_own = kv_own[None]
            kv_far = lax.ppermute(kv_own, 'tp', swap)
            len_g = jnp.broadcast_to(lax.dynamic_slice(lens[:, g], (chip,), (1,)), (quarter,))
            context = attend(q_rot, (kv_own, kv_far), 1, seq_dev, start1, keys1, len_g, groups, head_dim)
            hidden[g] = add_out(hidden[g], context, weights[3])
            before = hidden[g]
            wide[g] = lax.all_gather(hidden[g], 'tp', axis=0, tiled=True).reshape(n_dev * n_chip, seq_dev, d_model)

        total = [mlp(wide[g], 1, n_dev) for g in streams]
        outs = []
        for g in streams:
            mine = lax.dynamic_slice(wide[g].reshape(n_chip, n_dev, seq_dev, d_model), (0, me, 0, 0), (n_chip, 1, seq_dev, d_model))
            last = (mine.reshape(n_chip, seq_dev, d_model).astype(jnp.float32) + total[g].reshape(n_chip, seq_dev, d_model)).astype(jnp.bfloat16)
            outs.append(rms_norm(last, final_norm))
        return jnp.stack(outs, axis=1).reshape(batch, seq_dev, d_model)

    seq_part = P(None, 'tp', None)
    in_specs = (seq_part, P(), P(), P(), P(), P(), P(), P(), P(None, None, 'tp'), P(None, None, 'tp'), P(None, 'tp', None), P())
    return jax.shard_map(device_fn, mesh=mesh, in_specs=in_specs, out_specs=seq_part, check_vma=False)
```

time: 4270 us -> 2810 us (0.66)
  waiting for transfers between devices: 1490 us -> 520 us
  blocking collectives: 832 us -> 0 us
  Pallas kernels: 0 us -> 393 us
  other arithmetic: 410 us -> 138 us
  local copies, waits for them, and re-layouts: 162 us -> 370 us
    all_to_all x1 -> x0, blocking collectives: 832 us -> none  [device_fn(): received = lax.all_to_all(part_out, 'tp', 1, 1, tiled=True)]
    all_to_all x1 -> x0, waiting for transfers between devices: 814 us -> none  [device_fn(): received = lax.all_to_all(part_out, 'tp', 1, 1, tiled=True)]
    all_gather x6 -> x9, waiting for transfers between devices: 677 us -> 16.6 us  [the longest x6 16.6 us: device_fn(): lax.all_gather(hidden[g], 'tp', axis=0, tiled=True)]
    reduce_scatter x0 -> x6, waiting for transfers between devices: none -> 503 us  [mlp(): lax.psum_scatter(part_out.reshape(n_dev, -1, d_model), 'tp', scatter_dime...]
    pallas_call x0 -> x12, Pallas kernels: none -> 393 us  [the longest x6 200 us: attend(): pl.pallas_call(functools.partial(attend_kernel, groups, head_dim), grid_s...]
    sub x2 -> x0, other arithmetic: 226 us -> none  [attend(): prob_mat = jax.nn.softmax(scores, axis=-1).astype(jnp.bfloat16)]
    unnamed x0 -> x15, matrix products: none -> 199 us
    dot_general x18 -> x27, matrix products: 1340 us -> 1150 us  [the longest x6 336 us: mlp(): jnp.dot(gated_act, w_down[layer], preferred_element_type=jnp.float32)]
  transfers between devices with their start and end apart: 7 -> 18, of which waited for: 4 -> 4; matrix products, arithmetic and copies ran while one was open for 13% -> 63% of each run, Pallas kernels for 0% -> 14%
where the time goes in v1:
time: 2810 us; the launch traced here: 2790 us
  matrix products  1350 us (48%)
  waiting for transfers between devices  520 us (19%)
  Pallas kernels  393 us (14%)
  local copies, waits for them, and re-layouts  370 us (13%)
  other arithmetic  138 us (5%)
    reduce_scatter x6, waiting for transfers between devices, mlp(): lax.psum_scatter(part_out.reshape(n_dev, -1, d_model), 'tp', scatter_dime...  503 us
    dot_general x6, matrix products, mlp(): jnp.dot(gated_act, w_down[layer], preferred_element_type=jnp.float32)  336 us
    dot_general x6, matrix products, mlp(): up_proj = jnp.dot(normed, w_up[layer], preferred_element_type=jnp.float32)  335 us
    dot_general x6, matrix products, mlp(): jnp.dot(normed, w_gate[layer], preferred_element_type=jnp.float32)  333 us
    pallas_call x6, Pallas kernels, attend(): pl.pallas_call(functools.partial(attend_kernel, groups, head_dim), grid_s...  200 us
    unnamed x15, matrix products  199 us
    pallas_call x6, Pallas kernels, norm_rows(): pl.pallas_call(norm_kernel, grid=(n,), in_specs=[pl.BlockSpec((1, rows, w...  193 us
    dot_general x6, matrix products, add_out(): attn_out = jnp.dot(context, w_mat, preferred_element_type=jnp.float32)  130 us
  transfers between devices with their start and end apart: 18, of which 4 were waited for; matrix products, arithmetic and copies ran while one was open for 63% of the time, Pallas kernels for 14%

profile of v1, /device:TPU:0, one launch (start us, length us, event | category | flops | bytes accessed | tf_op | source)
XLA Modules:
  0.0 2790.5 jit_solution(7122695049116049398)
XLA Ops:
  150.3 42.7 %copy.80 = bf16[1,4096,32,128]{1,3,2,0:T(8,128)(2,1)} copy(bf16[1,4096,32,128]{3,2,1,0:T(8,128)(2,1)} %slice.172) | data formatting | bytes 67108864
  302.6 33.9 %attend.6 = bf16[384,4096]{1,0:T(8,128)(2,1)} custom-call(s32[4]{0:T(128)} %broadcast_in_dim.20.q_start, s32[2]{0:T(128)} %iota_multiply_fusion.k_start, s32[4]{0:T(128)} %get-tuple-element.20.lens, bf16[384,4096]{1,0:T(8,128)(2,1)} %copy.67.q_ref, bf16[4,768,2048]{2,1,0:T(8,128)(2,1)} %all-gather.10.cloned.1.call-done.ka_ref.kb_ref.va_ref.vb_ref, ...), custom_call_target="tpu_custom_call" | custom-call | flops 19327352832 | bytes 12582912 | tf_op jit(solution)/shard_map/attend/pallas_call | solution.py:93
  363.9 33.9 %attend.9 = bf16[384,4096]{1,0:T(8,128)(2,1)} custom-call(s32[4]{0:T(128)} %broadcast_in_dim.20.q_start, s32[2]{0:T(128)} %iota_multiply_fusion.k_start, s32[4]{0:T(128)} %get-tuple-element.22.lens, bf16[384,4096]{1,0:T(8,128)(2,1)} %copy.72.q_ref, bf16[4,768,2048]{2,1,0:T(8,128)(2,1)} %all-gather.20.cloned.1.call-done.ka_ref.kb_ref.va_ref.vb_ref, ...), custom_call_target="tpu_custom_call" | custom-call | flops 19327352832 | bytes 12582912 | tf_op jit(solution)/shard_map/attend/pallas_call | solution.py:93
  425.3 33.9 %attend.7 = bf16[384,4096]{1,0:T(8,128)(2,1)} custom-call(s32[4]{0:T(128)} %broadcast_in_dim.20.q_start, s32[2]{0:T(128)} %iota_multiply_fusion.k_start, s32[4]{0:T(128)} %get-tuple-element.21.lens, bf16[384,4096]{1,0:T(8,128)(2,1)} %copy.68.q_ref, bf16[4,768,2048]{2,1,0:T(8,128)(2,1)} %all-gather.14.cloned.1.call-done.ka_ref.kb_ref.va_ref.vb_ref, ...), custom_call_target="tpu_custom_call" | custom-call | flops 19327352832 | bytes 12582912 | tf_op jit(solution)/shard_map/attend/pallas_call | solution.py:93
  514.6 55.5 %fusion.22 = f32[3072,1792]{1,0:T(8,128)} fusion(bf16[3072,4096]{1,0:T(8,128)(2,1)} %bitcast.338, bf16[2,4096,1792]{2,1,0:T(8,128)(2,1)} %param.20), kind=kOutput, calls=%fused_computation.34 | convolution fusion | flops 45097156608 | bytes 61865984 | tf_op jit(solution)/shard_map/dot_general | solution.py:143
  570.0 55.8 %multiply_convert_fusion.5 = bf16[3072,1792]{1,0:T(8,128)(2,1)} fusion(f32[3072,1792]{1,0:T(8,128)} %fusion.22, bf16[3072,4096]{1,0:T(8,128)(2,1)} %bitcast.339, bf16[2,4096,1792]{2,1,0:T(8,128)(2,1)} %param.21), kind=kOutput, calls=%fused_computation.11 | convolution fusion | flops 45130186752 | bytes 72876032 | tf_op jit(solution)/shard_map/dot_general | solution.py:144
  625.9 56.0 %convolution_reduce-precision_fusion.5 = f32[3072,4096]{1,0:T(8,128)} fusion(bf16[3072,1792]{1,0:T(8,128)(2,1)} %multiply_convert_fusion.5, bf16[2,1792,4096]{2,1,0:T(8,128)(2,1)} %param.22), kind=kOutput, calls=%fused_computation.5 | convolution fusion | flops 45109739520 | bytes 76021760 | tf_op jit(solution)/shard_map/dot_general | solution.py:146
  681.9 32.3 %norm_rows.8 = bf16[32,96,4096]{2,1,0:T(8,128)(2,1)} custom-call(bf16[32,96,4096]{2,1,0:T(8,128)(2,1)} %bitcast.330, bf16[1,4096]{1,0:T(2,128)(2,1)} %get-tuple-element.71.gain_ref), custom_call_target="tpu_custom_call" | custom-call | flops 503316480 | bytes 50331648 | tf_op jit(solution)/shard_map/norm_rows/pallas_call | solution.py:41
  714.2 55.4 %fusion.20 = f32[3072,1792]{1,0:T(8,128)} fusion(bf16[3072,4096]{1,0:T(8,128)(2,1)} %bitcast.340, bf16[2,4096,1792]{2,1,0:T(8,128)(2,1)} %param.20), kind=kOutput, calls=%fused_computation.32 | convolution fusion | flops 45097156608 | bytes 61865984 | tf_op jit(solution)/shard_map/dot_general | solution.py:143
  769.6 55.8 %multiply_convert_fusion.3 = bf16[3072,1792]{1,0:T(8,128)(2,1)} fusion(f32[3072,1792]{1,0:T(8,128)} %fusion.20, bf16[3072,4096]{1,0:T(8,128)(2,1)} %bitcast.341, bf16[2,4096,1792]{2,1,0:T(8,128)(2,1)} %param.21), kind=kOutput, calls=%fused_computation.9 | convolution fusion | flops 45130186752 | bytes 72876032 | tf_op jit(solution)/shard_map/dot_general | solution.py:144
  825.5 56.2 %convolution_reduce-precision_fusion.3 = f32[3072,4096]{1,0:T(8,128)} fusion(bf16[3072,1792]{1,0:T(8,128)(2,1)} %multiply_convert_fusion.3, bf16[2,1792,4096]{2,1,0:T(8,128)(2,1)} %param.22), kind=kOutput, calls=%fused_computation.3 | convolution fusion | flops 45109739520 | bytes 76021760 | tf_op jit(solution)/shard_map/dot_general | solution.py:146
  881.8 32.2 %norm_rows.10 = bf16[32,96,4096]{2,1,0:T(8,128)(2,1)} custom-call(bf16[32,96,4096]{2,1,0:T(8,128)(2,1)} %bitcast.328, bf16[1,4096]{1,0:T(2,128)(2,1)} %get-tuple-element.71.gain_ref), custom_call_target="tpu_custom_call" | custom-call | flops 503316480 | bytes 50331648 | tf_op jit(solution)/shard_map/norm_rows/pallas_call | solution.py:41
  914.0 55.4 %fusion.18 = f32[3072,1792]{1,0:T(8,128)} fusion(bf16[3072,4096]{1,0:T(8,128)(2,1)} %bitcast.334, bf16[2,4096,1792]{2,1,0:T(8,128)(2,1)} %param.20), kind=kOutput, calls=%fused_computation.30 | convolution fusion | flops 45097156608 | bytes 61865984 | tf_op jit(solution)/shard_map/dot_general | solution.py:143
  969.5 55.8 %multiply_convert_fusion.1 = bf16[3072,1792]{1,0:T(8,128)(2,1)} fusion(f32[3072,1792]{1,0:T(8,128)} %fusion.18, bf16[3072,4096]{1,0:T(8,128)(2,1)} %bitcast.335, bf16[2,4096,1792]{2,1,0:T(8,128)(2,1)} %param.21), kind=kOutput, calls=%fused_computation.7 | convolution fusion | flops 45130186752 | bytes 72876032 | tf_op jit(solution)/shard_map/dot_general | solution.py:144
  1025.3 55.9 %convolution_reduce-precision_fusion.1 = f32[3072,4096]{1,0:T(8,128)} fusion(bf16[3072,1792]{1,0:T(8,128)(2,1)} %multiply_convert_fusion.1, bf16[2,1792,4096]{2,1,0:T(8,128)(2,1)} %param.22), kind=kOutput, calls=%fused_computation.1 | convolution fusion | flops 45109739520 | bytes 76021760 | tf_op jit(solution)/shard_map/dot_general | solution.py:146
  1166.7 84.1 %copy.51 = bf16[2,4096,32,128]{1,3,2,0:T(8,128)(2,1)} copy(bf16[2,4096,32,128]{3,2,1,0:T(8,128)(2,1)} %param.15) | data formatting | bytes 134217728 | tf_op jit(solution)/shard_map/optimization_barrier | solution.py:173
  1341.6 32.6 %attend.8 = bf16[384,4096]{1,0:T(8,128)(2,1)} custom-call(s32[4]{0:T(128)} %multiply_add_fusion.q_start, s32[2]{0:T(128)} %pad_add_fusion.k_start, s32[4]{0:T(128)} %broadcast_in_dim.22.lens, bf16[384,4096]{1,0:T(8,128)(2,1)} %copy.69.q_ref, bf16[1,384,2048]{2,1,0:T(8,128)(2,1)} %maximum_bitcast_fusion.ka_ref.va_ref, ...), custom_call_target="tpu_custom_call" | custom-call | flops 19327352832 | bytes 12582912 | tf_op jit(solution)/shard_map/attend/pallas_call | solution.py:93
  1449.7 32.6 %attend.10 = bf16[384,4096]{1,0:T(8,128)(2,1)} custom-call(s32[4]{0:T(128)} %multiply_add_fusion.q_start, s32[2]{0:T(128)} %pad_add_fusion.k_start, s32[4]{0:T(128)} %broadcast_in_dim.25.lens, bf16[384,4096]{1,0:T(8,128)(2,1)} %copy.73.q_ref, bf16[1,384,2048]{2,1,0:T(8,128)(2,1)} %maximum_bitcast_fusion.1.ka_ref.va_ref, ...), custom_call_target="tpu_custom_call" | custom-call | flops 19327352832 | bytes 12582912 | tf_op jit(solution)/shard_map/attend/pallas_call | solution.py:93
  1505.7 53.2 %reduce-scatter.15.cloned.1.call-done = f32[1,384,4096]{2,1,0:T(8,128)} async-done(((f32[8,384,4096]{2,1,0:T(8,128)}), f32[1,384,4096]{2,1,0:T(8,128)}) %reduce-scatter.15.cloned.1.call-update) | async-done | bytes 6291472 | tf_op jit(solution)/shard_map/reduce_scatter | solution.py:148
  1609.6 32.6 %attend.11 = bf16[384,4096]{1,0:T(8,128)(2,1)} custom-call(s32[4]{0:T(128)} %multiply_add_fusion.q_start, s32[2]{0:T(128)} %pad_add_fusion.k_start, s32[4]{0:T(128)} %broadcast_in_dim.28.lens, bf16[384,4096]{1,0:T(8,128)(2,1)} %copy.76.q_ref, bf16[1,384,2048]{2,1,0:T(8,128)(2,1)} %maximum_bitcast_fusion.2.ka_ref.va_ref, ...), custom_call_target="tpu_custom_call" | custom-call | flops 19327352832 | bytes 12582912 | tf_op jit(solution)/shard_map/attend/pallas_call | solution.py:93
  1712.2 55.5 %fusion.10 = f32[3072,1792]{1,0:T(8,128)} fusion(bf16[3072,4096]{1,0:T(8,128)(2,1)} %bitcast.342, bf16[2,4096,1792]{2,1,0:T(8,128)(2,1)} %param.20), kind=kOutput, calls=%fused_computation.22 | convolution fusion | flops 45097156608 | bytes 61865984 | tf_op jit(solution)/shard_map/dot_general | solution.py:143
  1767.7 56.2 %multiply_convert_fusion.4 = bf16[3072,1792]{1,0:T(8,128)(2,1)} fusion(f32[3072,1792]{1,0:T(8,128)} %fusion.10, bf16[3072,4096]{1,0:T(8,128)(2,1)} %bitcast.343, bf16[2,4096,1792]{2,1,0:T(8,128)(2,1)} %param.21), kind=kOutput, calls=%fused_computation.10 | convolution fusion | flops 45130186752 | bytes 72876032 | tf_op jit(solution)/shard_map/dot_general | solution.py:144
  1823.9 55.9 %convolution_reduce-precision_fusion.4 = f32[3072,4096]{1,0:T(8,128)} fusion(bf16[3072,1792]{1,0:T(8,128)(2,1)} %multiply_convert_fusion.4, bf16[2,1792,4096]{2,1,0:T(8,128)(2,1)} %param.22), kind=kOutput, calls=%fused_computation.4 | convolution fusion | flops 45109739520 | bytes 76021760 | tf_op jit(solution)/shard_map/dot_general | solution.py:146
  1912.1 55.5 %fusion.8 = f32[3072,1792]{1,0:T(8,128)} fusion(bf16[3072,4096]{1,0:T(8,128)(2,1)} %bitcast.344, bf16[2,4096,1792]{2,1,0:T(8,128)(2,1)} %param.20), kind=kOutput, calls=%fused_computation.20 | convolution fusion | flops 45097156608 | bytes 61865984 | tf_op jit(solution)/shard_map/dot_general | solution.py:143
  1967.7 55.9 %multiply_convert_fusion.2 = bf16[3072,1792]{1,0:T(8,128)(2,1)} fusion(f32[3072,1792]{1,0:T(8,128)} %fusion.8, bf16[3072,4096]{1,0:T(8,128)(2,1)} %bitcast.345, bf16[2,4096,1792]{2,1,0:T(8,128)(2,1)} %param.21), kind=kOutput, calls=%fused_computation.8 | convolution fusion | flops 45130186752 | bytes 72876032 | tf_op jit(solution)/shard_map/dot_general | solution.py:144
  2023.5 56.3 %convolution_reduce-precision_fusion.2 = f32[3072,4096]{1,0:T(8,128)} fusion(bf16[3072,1792]{1,0:T(8,128)(2,1)} %multiply_convert_fusion.2, bf16[2,1792,4096]{2,1,0:T(8,128)(2,1)} %param.22), kind=kOutput, calls=%fused_computation.2 | convolution fusion | flops 45109739520 | bytes 76021760 | tf_op jit(solution)/shard_map/dot_general | solution.py:146
  2079.9 32.2 %norm_rows.11 = bf16[32,96,4096]{2,1,0:T(8,128)(2,1)} custom-call(bf16[32,96,4096]{2,1,0:T(8,128)(2,1)} %bitcast.313, bf16[1,4096]{1,0:T(2,128)(2,1)} %get-tuple-element.70.gain_ref), custom_call_target="tpu_custom_call" | custom-call | flops 503316480 | bytes 50331648 | tf_op jit(solution)/shard_map/norm_rows/pallas_call | solution.py:41
  2112.1 55.5 %fusion.6 = f32[3072,1792]{1,0:T(8,128)} fusion(bf16[3072,4096]{1,0:T(8,128)(2,1)} %bitcast.336, bf16[2,4096,1792]{2,1,0:T(8,128)(2,1)} %param.20), kind=kOutput, calls=%fused_computation.18 | convolution fusion | flops 45097156608 | bytes 61865984 | tf_op jit(solution)/shard_map/dot_general | solution.py:143
  2167.6 55.8 %multiply_convert_fusion = bf16[3072,1792]{1,0:T(8,128)(2,1)} fusion(f32[3072,1792]{1,0:T(8,128)} %fusion.6, bf16[3072,4096]{1,0:T(8,128)(2,1)} %bitcast.337, bf16[2,4096,1792]{2,1,0:T(8,128)(2,1)} %param.21), kind=kOutput, calls=%fused_computation.6 | convolution fusion | flops 45130186752 | bytes 72876032 | tf_op jit(solution)/shard_map/dot_general | solution.py:144
  2223.4 56.2 %convolution_reduce-precision_fusion = f32[3072,4096]{1,0:T(8,128)} fusion(bf16[3072,1792]{1,0:T(8,128)(2,1)} %multiply_convert_fusion, bf16[2,1792,4096]{2,1,0:T(8,128)(2,1)} %param.22), kind=kOutput, calls=%fused_computation | convolution fusion | flops 45109739520 | bytes 76021760 | tf_op jit(solution)/shard_map/dot_general | solution.py:146
  2301.6 177.4 %reduce-scatter.13.cloned.1.call-done = f32[1,384,4096]{2,1,0:T(8,128)} async-done(((f32[8,384,4096]{2,1,0:T(8,128)}), f32[1,384,4096]{2,1,0:T(8,128)}) %reduce-scatter.13.cloned.1.call-update) | async-done | bytes 6291472 | tf_op jit(solution)/shard_map/reduce_scatter | solution.py:148
  2484.5 272.6 %reduce-scatter.17.cloned.1.call-done = f32[1,384,4096]{2,1,0:T(8,128)} async-done(((f32[8,384,4096]{2,1,0:T(8,128)}), f32[1,384,4096]{2,1,0:T(8,128)}) %reduce-scatter.17.cloned.1.call-update) | async-done | bytes 6291472 | tf_op jit(solution)/shard_map/reduce_scatter | solution.py:148
  (239 shorter events, 845.0 us)
Async XLA Ops:
  6.5 295.6 %all-gather.10.cloned.1.call-start = ((), (), s32[]{:S(2)}) async-start(), calls=%async_computation.6 | async-start | bytes 14155776 | tf_op jit(solution)/shard_map/all_gather | solution.py:166
  12.1 11.3 copy-start.1
  46.4 18.8 copy-start.5
  57.2 15.4 slice-start
  80.3 8.6 copy-start.8
  88.8 275.1 %all-gather.20.cloned.1.call-start = ((), (), s32[]{:S(2)}) async-start(), calls=%async_computation.13 | async-start | bytes 14155776 | tf_op jit(solution)/shard_map/all_gather | solution.py:166
  95.0 13.1 copy-start.6
  108.0 317.3 %all-gather.14.cloned.1.call-start = ((), (), s32[]{:S(2)}) async-start(), calls=%async_computation.9 | async-start | bytes 14155776 | tf_op jit(solution)/shard_map/all_gather | solution.py:166
  114.2 12.9 copy-start.22
  127.0 355.5 %all-gather.12.cloned.1.call-start = ((), (), s32[]{:S(2)}) async-start(), calls=%async_computation.7 | async-start | bytes 28311552 | tf_op jit(solution)/shard_map/all_gather | solution.py:169
  236.8 22.4 copy-start.15
  236.9 22.4 copy-start.17
  358.7 323.2 %all-gather.22.cloned.1.call-start = ((), (), s32[]{:S(2)}) async-start(), calls=%async_computation.14 | async-start | bytes 28311552 | tf_op jit(solution)/shard_map/all_gather | solution.py:169
  420.0 461.8 %all-gather.16.cloned.1.call-start = ((), (), s32[]{:S(2)}) async-start(), calls=%async_computation.10 | async-start | bytes 28311552 | tf_op jit(solution)/shard_map/all_gather | solution.py:169
  459.2 22.6 copy-start.20
  481.4 797.6 %reduce-scatter.7.cloned.1.call-start = ((), (), s32[]{:S(2)}) async-start(), calls=%async_computation.8 | async-start | bytes 56623104 | tf_op jit(solution)/shard_map/reduce_scatter | solution.py:148
  681.9 717.0 %reduce-scatter.11.cloned.1.call-start = ((), (), s32[]{:S(2)}) async-start(), calls=%async_computation.15 | async-start | bytes 56623104 | tf_op jit(solution)/shard_map/reduce_scatter | solution.py:148
  881.7 677.1 %reduce-scatter.15.cloned.1.call-start = ((), (), s32[]{:S(2)}) async-start(), calls=%async_computation.18 | async-start | bytes 56623104 | tf_op jit(solution)/shard_map/reduce_scatter | solution.py:148
  1081.3 598.9 %all-gather.18.cloned.1.call-start = ((), (), s32[]{:S(2)}) async-start(), calls=%async_computation.11 | async-start | bytes 28311552 | tf_op jit(solution)/shard_map/all_gather | solution.py:187
  1279.0 9.4 copy-start.2
  1313.6 26.8 collective-permute-start
  1341.6 32.6 %copy-start.9 = (bf16[384,4096]{1,0:T(8,128)(2,1)S(1)}, bf16[384,4096]{1,0:T(8,128)(2,1)}, u32[]{:S(2)}) copy-start(bf16[384,4096]{1,0:T(8,128)(2,1)} %get-tuple-element.28) | copy-start | bytes 9437188
  1395.4 484.5 %all-gather.24.cloned.1.call-start = ((), (), s32[]{:S(2)}) async-start(), calls=%async_computation.16 | async-start | bytes 28311552 | tf_op jit(solution)/shard_map/all_gather | solution.py:187
  1421.5 27.0 collective-permute-start.1
  1449.7 32.6 %copy-start.13 = (bf16[384,4096]{1,0:T(8,128)(2,1)S(1)}, bf16[384,4096]{1,0:T(8,128)(2,1)}, u32[]{:S(2)}) copy-start(bf16[384,4096]{1,0:T(8,128)(2,1)} %copy-done.12) | copy-start | bytes 9437188
  1503.5 576.4 %all-gather.26.cloned.1.call-start = ((), (), s32[]{:S(2)}) async-start(), calls=%async_computation.19 | async-start | bytes 28311552 | tf_op jit(solution)/shard_map/all_gather | solution.py:187
  1562.9 8.2 copy-start.10
  1581.5 26.9 collective-permute-start.2
  1609.6 32.6 %copy-start.11 = (bf16[384,4096]{1,0:T(8,128)(2,1)S(1)}, bf16[384,4096]{1,0:T(8,128)(2,1)}, u32[]{:S(2)}) copy-start(bf16[384,4096]{1,0:T(8,128)(2,1)} %copy-done.10) | copy-start | bytes 9437188
  1663.6 632.7 %reduce-scatter.9.cloned.1.call-start = ((), (), s32[]{:S(2)}) async-start(), calls=%async_computation.12 | async-start | bytes 56623104 | tf_op jit(solution)/shard_map/reduce_scatter | solution.py:148
  1879.9 599.2 %reduce-scatter.13.cloned.1.call-start = ((), (), s32[]{:S(2)}) async-start(), calls=%async_computation.17 | async-start | bytes 56623104 | tf_op jit(solution)/shard_map/reduce_scatter | solution.py:148
  2079.8 677.3 %reduce-scatter.17.cloned.1.call-start = ((), (), s32[]{:S(2)}) async-start(), calls=%async_computation.20 | async-start | bytes 56623104 | tf_op jit(solution)/shard_map/reduce_scatter | solution.py:148
  (11 other events, 60.8 us)
Sparse Core Ops, SparseCore 0:
  88.9 69.1 all-gather.9
  159.9 66.2 all-gather.19
  228.1 66.2 all-gather.13
  358.8 122.4 all-gather.11
  483.0 119.6 all-gather.21
  604.3 119.6 all-gather.15
  727.6 274.5 reduce-scatter.6
  1005.7 274.5 reduce-scatter.10
  1283.8 274.9 reduce-scatter.14
  1560.5 119.6 all-gather.17
  1682.0 119.6 all-gather.23
  1803.3 119.6 all-gather.25
  1926.6 274.5 reduce-scatter.8
  2204.5 274.5 reduce-scatter.12
  2482.5 274.5 reduce-scatter.16
